TPU v7x, 256 devices: a whole 4x4x8 slice. The times are simulated.
256 devices in a mesh: grp: 16 (over z, core), sub: 16 (over x, y).
Axes of the slice: x: 4, y: 4, z: 8, core: 2. Of those that a mesh axis runs over, the one named last changes fastest.
Arguments:
- coarse_op: float32 [256, 64, 576], P(('grp', 'sub'))
- right_side: float32 [256, 64, 64], P(('grp', 'sub')), may hold values from -6 to 6
- owner_map: int32 [256], replicated, may hold values from 0 to 255, as said below
- neighbor_table: int32 [256, 8], replicated, may hold values from 0 to 255, as said below
Outputs:
- solution: float32 [256, 64, 64], P(('grp', 'sub'))
Inputs may be any that keep to these rules, and one draw needn't show every extreme that they name: `owner_map`: a permutation of 0 .. 255. `neighbor_table`: row t lists the neighbours of coarse site t on a periodic 4^4 lattice in the order +x, -x, +y, -y, +z, -z, +t, -t; lattice positions carry the site numbers in a permuted order.
All inputs are finite; a program needn't handle non-finite values.
Results may differ from a plain program's by a relative error of at most 0.0001.
Values sent between devices are 32-bit elements; how exact they have to be, the bound alone decides.
A program may use at most 64 MiB of HBM per device.

v0:
```python
import jax
import jax.numpy as jnp
from jax import lax
from jax.sharding import PartitionSpec as P

ITERS = 3


def from_everyone(array, axis):
    copies = jnp.broadcast_to(array, (lax.axis_size(axis), *array.shape))
    return lax.all_to_all(copies, axis, split_axis=0, concat_axis=0, tiled=True)


def laid_out(parts, dim):
    parts = jnp.moveaxis(parts, 0, dim)
    shape = parts.shape
    return parts.reshape(*shape[:dim], shape[dim] * shape[dim + 1], *shape[dim + 2 :])


def gathered_copies(array, axis, dim):
    parts = from_everyone(array, axis)
    return laid_out(parts, dim)


def over_copies(array, axis):
    return from_everyone(array, axis).sum(axis=0)


def inner_product(first, second):
    return jnp.sum(first * second, axis=(0, 1))


def per_device(coarse_op, right_side, owner_map, neighbor_table):
    n_sub = lax.axis_size("sub")
    n_grp = lax.axis_size("grp")
    per_dev = coarse_op.shape[0]
    dof_count = coarse_op.shape[1]
    site_count = owner_map.shape[0]
    site_ids = jnp.arange(site_count, dtype=jnp.int32)
    inverse = jnp.sum(
        jnp.where(owner_map[None, :] == site_ids[:, None], site_ids[None, :], 0), axis=1
    )
    link = inverse[neighbor_table[owner_map]]
    op_rows = lax.all_gather(coarse_op, "grp", axis=0, tiled=True)
    rhs_rows = lax.all_to_all(right_side, "grp", split_axis=2, concat_axis=0, tiled=True)

    def reduce_sum(values):
        return jax.tree.map(lambda part: over_copies(part, "sub"), values)

    row_count = op_rows.shape[0]
    local_rows = jnp.arange(row_count, dtype=jnp.int32)
    own_slots = (
        local_rows // per_dev * n_sub + lax.axis_index("sub")
    ) * per_dev + local_rows % per_dev
    target = link[own_slots]
    target_block = target // per_dev
    position = (target_block % n_sub * n_grp + target_block // n_sub) * per_dev + target % per_dev
    rhs_count = rhs_rows.shape[2]
    beta = jnp.sqrt(reduce_sum(inner_product(rhs_rows, rhs_rows)))
    krylov = [rhs_rows / beta]
    hess = jnp.zeros((ITERS + 1, ITERS, rhs_count), jnp.float32)
    for column in range(ITERS):
        apply_vector = krylov[column]
        piece = gathered_copies(apply_vector, "sub", 0)
        count = piece.shape[0]
        select = (position[:, :, None] == jnp.arange(count, dtype=jnp.int32)[None, None, :]).astype(
            jnp.float32
        )
        nearby = jnp.einsum("lkr,rab->lkab", select, piece, precision=lax.Precision.HIGHEST)
        stacked = jnp.concatenate([apply_vector[:, None], nearby], axis=1).reshape(
            row_count, 9 * dof_count, rhs_count
        )
        image = jnp.einsum("sac,scr->sar", op_rows, stacked, precision=lax.Precision.HIGHEST)
        totals = reduce_sum(
            tuple(
                [inner_product(vector, image) for vector in krylov] + [inner_product(image, image)]
            )
        )
        norm_sq = totals[-1]
        for index_i in range(column + 1):
            image = image - totals[index_i] * krylov[index_i]
            hess = hess.at[index_i, column].set(totals[index_i])
            norm_sq = norm_sq - totals[index_i] * totals[index_i]
        norm_value = jnp.sqrt(norm_sq)
        hess = hess.at[column + 1, column].set(norm_value)
        krylov.append(image / norm_value)
    gram_matrix = jnp.einsum("ijr,ikr->rjk", hess, hess, precision=lax.Precision.HIGHEST)
    projected = (beta[None, :] * hess[0]).T
    factor = jnp.linalg.cholesky(gram_matrix)
    halfway = jax.scipy.linalg.solve_triangular(factor, projected[..., None], lower=True)
    weights = jax.scipy.linalg.solve_triangular(factor, halfway, lower=True, trans=1)[..., 0]
    solution = jnp.zeros_like(rhs_rows)
    for column in range(ITERS):
        solution = solution + weights[:, column][None, None, :] * krylov[column]
    return lax.all_to_all(solution, "grp", split_axis=0, concat_axis=2, tiled=True)


def solution(mesh):
    placed = (P(("grp", "sub"), None, None), P(("grp", "sub"), None, None), P(), P())
    return jax.shard_map(
        per_device,
        mesh=mesh,
        in_specs=placed,
        out_specs=P(("grp", "sub"), None, None),
        check_vma=False,
    )
```

profile of v0, /device:TPU:1, one launch (start us, length us, event | category | flops | bytes accessed | tf_op | source)
XLA Modules:
  0.0 240.6 jit_solution(6348703550296950979)
XLA Ops:
  10.1 10.0 %all-to-all-start = ((f32[16,1,256]{2,1,0:T(1,128)}), f32[16,1,256]{2,1,0:T(1,128)S(1)}, u32[]{:S(2)}, u32[]{:S(2)}) async-start(f32[16,1,256]{2,1,0:T(1,128)} %reshape.567), calls=%async_computation | async-start | bytes 32768 | tf_op jit(solution)/shard_map/all_to_all | solution.py:45
  23.3 4.1 %all-to-all-done = f32[16,1,256]{2,1,0:T(1,128)S(1)} async-done(((f32[16,1,256]{2,1,0:T(1,128)}), f32[16,1,256]{2,1,0:T(1,128)S(1)}, u32[]{:S(2)}, u32[]{:S(2)}) %all-to-all-start) | async-done | bytes 16416 | tf_op jit(solution)/shard_map/all_to_all | solution.py:45
  29.0 6.8 %all-to-all-start.1 = ((f32[16,1,4]{2,1,0:T(1,128)}), f32[16,1,4]{2,1,0:T(1,128)S(1)}, u32[]{:S(2)}, u32[]{:S(2)}) async-start(f32[16,1,4]{2,1,0:T(1,128)} %broadcast_in_dim.48), calls=%async_computation.1 | async-start | bytes 16384 | tf_op jit(solution)/shard_map/all_to_all | solution.py:11
  35.8 13.1 %gather_fusion.1 = s32[2048]{0:T(1024)S(1)} fusion(s32[256]{0:T(256)S(1)} %select_reduce_fusion, s32[2048]{0:T(1024)S(1)} %broadcast_clamp_fusion), kind=kCustom, calls=%fused_computation.1 | custom fusion | bytes 24576 | tf_op jit(solution)/shard_map/gather | solution.py:43
  50.8 6.7 %all-to-all-start.2 = ((f32[16,1,4096]{2,1,0:T(1,128)}), f32[16,1,4096]{2,1,0:T(1,128)S(1)}, u32[]{:S(2)}, u32[]{:S(2)}) async-start(f32[16,1,4096]{2,1,0:T(1,128)} %reshape.569), calls=%async_computation.2 | async-start | bytes 524288 | tf_op jit(solution)/shard_map/all_to_all | solution.py:11
  57.6 7.3 %all-to-all-done.2 = f32[16,1,4096]{2,1,0:T(1,128)S(1)} async-done(((f32[16,1,4096]{2,1,0:T(1,128)}), f32[16,1,4096]{2,1,0:T(1,128)S(1)}, u32[]{:S(2)}, u32[]{:S(2)}) %all-to-all-start.2) | async-done | bytes 262176 | tf_op jit(solution)/shard_map/all_to_all | solution.py:11
  67.1 4.5 %multiply_reduce_fusion.8 = (f32[4]{0:T(128)S(1)}, f32[4]{0:T(128)S(1)}, f32[16,64,4]{1,2,0:T(4,128)S(1)}) fusion(f32[16,64,4]{1,2,0:T(4,128)S(1)} %broadcast_divide_fusion.1, f32[16,576,4]{1,2,0:T(4,128)S(1)} %reshape.564, f32[16,64,576]{2,1,0:T(8,128)} %all-gather.2.cloned.1.call-done), kind=kOutput, calls=%fused_computation.31 | convolution fusion | flops 28327928 | bytes 2539552 | tf_op jit(solution)/shard_map/sac,scr->sar/dot_general | solution.py:73
  71.6 9.8 %all_to_all.111 = f32[16,1,4]{2,1,0:T(1,128)S(1)} all-to-all(f32[16,1,4]{2,1,0:T(1,128)S(1)} %broadcast_in_dim.90), channel_id=1, replica_groups=mesh['grp'=16,'sub'=16] {'sub'}, dimensions={0} | all-to-all | bytes 512 | tf_op jit(solution)/shard_map/all_to_all | solution.py:11
  85.6 6.3 %all-to-all-done.4 = f32[16,1,4]{2,1,0:T(1,128)S(1)} async-done(((f32[16,1,4]{2,1,0:T(1,128)}), f32[16,1,4]{2,1,0:T(1,128)S(1)}, u32[]{:S(2)}, u32[]{:S(2)}) %all-to-all-start.4) | async-done | bytes 288 | tf_op jit(solution)/shard_map/all_to_all | solution.py:11
  93.0 3.8 %all-to-all-start.5 = ((f32[16,1,4096]{2,1,0:T(1,128)}), f32[16,1,4096]{2,1,0:T(1,128)S(1)}, u32[]{:S(2)}, u32[]{:S(2)}) async-start(f32[16,1,4096]{2,1,0:T(1,128)} %reshape.571), calls=%async_computation.5 | async-start | bytes 524288 | tf_op jit(solution)/shard_map/all_to_all | solution.py:11
  97.6 6.6 %all-to-all-done.5 = f32[16,1,4096]{2,1,0:T(1,128)S(1)} async-done(((f32[16,1,4096]{2,1,0:T(1,128)}), f32[16,1,4096]{2,1,0:T(1,128)S(1)}, u32[]{:S(2)}, u32[]{:S(2)}) %all-to-all-start.5) | async-done | bytes 262176 | tf_op jit(solution)/shard_map/all_to_all | solution.py:11
  109.7 3.5 %all-to-all-start.6 = ((f32[16,1,4]{2,1,0:T(1,128)}), f32[16,1,4]{2,1,0:T(1,128)S(1)}, u32[]{:S(2)}, u32[]{:S(2)}) async-start(f32[16,1,4]{2,1,0:T(1,128)} %broadcast_in_dim.94), calls=%async_computation.6 | async-start | bytes 16384 | tf_op jit(solution)/shard_map/all_to_all | solution.py:11
  113.9 5.7 %all-to-all-done.6 = f32[16,1,4]{2,1,0:T(1,128)S(1)} async-done(((f32[16,1,4]{2,1,0:T(1,128)}), f32[16,1,4]{2,1,0:T(1,128)S(1)}, u32[]{:S(2)}, u32[]{:S(2)}) %all-to-all-start.6) | async-done | bytes 288 | tf_op jit(solution)/shard_map/all_to_all | solution.py:11
  120.1 3.5 %all-to-all-start.7 = ((f32[16,1,4]{2,1,0:T(1,128)}), f32[16,1,4]{2,1,0:T(1,128)S(1)}, u32[]{:S(2)}, u32[]{:S(2)}) async-start(f32[16,1,4]{2,1,0:T(1,128)} %broadcast_in_dim.95), calls=%async_computation.7 | async-start | bytes 16384 | tf_op jit(solution)/shard_map/all_to_all | solution.py:11
  124.3 5.6 %all-to-all-done.7 = f32[16,1,4]{2,1,0:T(1,128)S(1)} async-done(((f32[16,1,4]{2,1,0:T(1,128)}), f32[16,1,4]{2,1,0:T(1,128)S(1)}, u32[]{:S(2)}, u32[]{:S(2)}) %all-to-all-start.7) | async-done | bytes 288 | tf_op jit(solution)/shard_map/all_to_all | solution.py:11
  130.5 3.7 %all-to-all-start.8 = ((f32[16,1,4]{2,1,0:T(1,128)}), f32[16,1,4]{2,1,0:T(1,128)S(1)}, u32[]{:S(2)}, u32[]{:S(2)}) async-start(f32[16,1,4]{2,1,0:T(1,128)} %broadcast_in_dim.96), calls=%async_computation.8 | async-start | bytes 16384 | tf_op jit(solution)/shard_map/all_to_all | solution.py:11
  134.7 5.7 %all-to-all-done.8 = f32[16,1,4]{2,1,0:T(1,128)S(1)} async-done(((f32[16,1,4]{2,1,0:T(1,128)}), f32[16,1,4]{2,1,0:T(1,128)S(1)}, u32[]{:S(2)}, u32[]{:S(2)}) %all-to-all-start.8) | async-done | bytes 288 | tf_op jit(solution)/shard_map/all_to_all | solution.py:11
  142.2 3.5 %all-to-all-start.9 = ((f32[16,1,4096]{2,1,0:T(1,128)}), f32[16,1,4096]{2,1,0:T(1,128)S(1)}, u32[]{:S(2)}, u32[]{:S(2)}) async-start(f32[16,1,4096]{2,1,0:T(1,128)} %reshape.573), calls=%async_computation.9 | async-start | bytes 524288 | tf_op jit(solution)/shard_map/all_to_all | solution.py:11
  146.9 6.2 %all-to-all-done.9 = f32[16,1,4096]{2,1,0:T(1,128)S(1)} async-done(((f32[16,1,4096]{2,1,0:T(1,128)}), f32[16,1,4096]{2,1,0:T(1,128)S(1)}, u32[]{:S(2)}, u32[]{:S(2)}) %all-to-all-start.9) | async-done | bytes 262176 | tf_op jit(solution)/shard_map/all_to_all | solution.py:11
  162.2 6.2 %all-to-all-done.10 = f32[16,1,4]{2,1,0:T(1,128)S(1)} async-done(((f32[16,1,4]{2,1,0:T(1,128)}), f32[16,1,4]{2,1,0:T(1,128)S(1)}, u32[]{:S(2)}, u32[]{:S(2)}) %all-to-all-start.10) | async-done | bytes 288 | tf_op jit(solution)/shard_map/all_to_all | solution.py:11
  172.6 6.3 %all-to-all-done.11 = f32[16,1,4]{2,1,0:T(1,128)S(1)} async-done(((f32[16,1,4]{2,1,0:T(1,128)}), f32[16,1,4]{2,1,0:T(1,128)S(1)}, u32[]{:S(2)}, u32[]{:S(2)}) %all-to-all-start.11) | async-done | bytes 288 | tf_op jit(solution)/shard_map/all_to_all | solution.py:11
  184.4 4.9 %all-to-all-done.12 = f32[16,1,4]{2,1,0:T(1,128)S(1)} async-done(((f32[16,1,4]{2,1,0:T(1,128)}), f32[16,1,4]{2,1,0:T(1,128)S(1)}, u32[]{:S(2)}, u32[]{:S(2)}) %all-to-all-start.12) | async-done | bytes 288 | tf_op jit(solution)/shard_map/all_to_all | solution.py:11
  193.5 6.2 %all-to-all-done.13 = f32[16,1,4]{2,1,0:T(1,128)S(1)} async-done(((f32[16,1,4]{2,1,0:T(1,128)}), f32[16,1,4]{2,1,0:T(1,128)S(1)}, u32[]{:S(2)}, u32[]{:S(2)}) %all-to-all-start.13) | async-done | bytes 288 | tf_op jit(solution)/shard_map/all_to_all | solution.py:11
  206.9 25.4 %all_to_all.112 = f32[16,1,256]{2,1,0:T(1,128)S(1)} all-to-all(f32[16,1,256]{2,1,0:T(1,128)S(1)} %reshape.575), channel_id=1, replica_groups=mesh['grp'=16,'sub'=16] {'grp'}, dimensions={0} | all-to-all | bytes 32768 | tf_op jit(solution)/shard_map/all_to_all | solution.py:95
  (156 shorter events, 61.4 us)
Async XLA Ops:
  6.5 60.6 %all-gather.2.cloned.1.call-start = ((), (), s32[]{:S(2)}) async-start(), calls=%async_computation.15 | async-start | bytes 2785280 | tf_op jit(solution)/shard_map/all_gather | solution.py:44
  10.1 17.3 %all-to-all-start = ((f32[16,1,256]{2,1,0:T(1,128)}), f32[16,1,256]{2,1,0:T(1,128)S(1)}, u32[]{:S(2)}, u32[]{:S(2)}) async-start(f32[16,1,256]{2,1,0:T(1,128)} %reshape.567), calls=%async_computation | async-start | bytes 32768 | tf_op jit(solution)/shard_map/all_to_all | solution.py:45
  29.0 20.6 %all-to-all-start.1 = ((f32[16,1,4]{2,1,0:T(1,128)}), f32[16,1,4]{2,1,0:T(1,128)S(1)}, u32[]{:S(2)}, u32[]{:S(2)}) async-start(f32[16,1,4]{2,1,0:T(1,128)} %broadcast_in_dim.48), calls=%async_computation.1 | async-start | bytes 16384 | tf_op jit(solution)/shard_map/all_to_all | solution.py:11
  50.8 14.1 %all-to-all-start.2 = ((f32[16,1,4096]{2,1,0:T(1,128)}), f32[16,1,4096]{2,1,0:T(1,128)S(1)}, u32[]{:S(2)}, u32[]{:S(2)}) async-start(f32[16,1,4096]{2,1,0:T(1,128)} %reshape.569), calls=%async_computation.2 | async-start | bytes 524288 | tf_op jit(solution)/shard_map/all_to_all | solution.py:11
  67.1 29.8 %copy-start.12 = (s32[3]{0:T(128)S(1)}, s32[3]{0:T(128)}, u32[]{:S(2)}) copy-start(s32[3]{0:T(128)} %constant.391.clone.1) | copy-start | bytes 40
  82.0 9.8 %all-to-all-start.4 = ((f32[16,1,4]{2,1,0:T(1,128)}), f32[16,1,4]{2,1,0:T(1,128)S(1)}, u32[]{:S(2)}, u32[]{:S(2)}) async-start(f32[16,1,4]{2,1,0:T(1,128)} %broadcast_in_dim.91), calls=%async_computation.4 | async-start | bytes 16384 | tf_op jit(solution)/shard_map/all_to_all | solution.py:11
  85.5 12.0 %copy-start.3 = (f32[4]{0:T(128)}, f32[4]{0:T(128)S(1)}, u32[]{:S(2)}) copy-start(f32[4]{0:T(128)S(1)} %reduce_sum.199) | copy-start | bytes 52
  93.0 13.3 %copy-start = (f32[16,64,576]{2,1,0:T(8,128)S(1)}, f32[16,64,576]{2,1,0:T(8,128)}, u32[]{:S(2)}) copy-start(f32[16,64,576]{2,1,0:T(8,128)} %all-gather.2.cloned.1.call-done) | copy-start | bytes 7077892
  93.0 11.1 %all-to-all-start.5 = ((f32[16,1,4096]{2,1,0:T(1,128)}), f32[16,1,4096]{2,1,0:T(1,128)S(1)}, u32[]{:S(2)}, u32[]{:S(2)}) async-start(f32[16,1,4096]{2,1,0:T(1,128)} %reshape.571), calls=%async_computation.5 | async-start | bytes 524288 | tf_op jit(solution)/shard_map/all_to_all | solution.py:11
  106.3 40.0 %copy-start.4 = (f32[4]{0:T(128)S(1)}, f32[4]{0:T(128)}, u32[]{:S(2)}) copy-start(f32[4]{0:T(128)} %copy-done.3) | copy-start | bytes 52
  106.3 40.0 %copy-start.10 = (f32[4]{0:T(128)S(1)}, f32[4]{0:T(128)}, u32[]{:S(2)}) copy-start(f32[4]{0:T(128)} %copy-done.9) | copy-start | bytes 52
  109.7 9.8 %all-to-all-start.6 = ((f32[16,1,4]{2,1,0:T(1,128)}), f32[16,1,4]{2,1,0:T(1,128)S(1)}, u32[]{:S(2)}, u32[]{:S(2)}) async-start(f32[16,1,4]{2,1,0:T(1,128)} %broadcast_in_dim.94), calls=%async_computation.6 | async-start | bytes 16384 | tf_op jit(solution)/shard_map/all_to_all | solution.py:11
  120.1 9.8 %all-to-all-start.7 = ((f32[16,1,4]{2,1,0:T(1,128)}), f32[16,1,4]{2,1,0:T(1,128)S(1)}, u32[]{:S(2)}, u32[]{:S(2)}) async-start(f32[16,1,4]{2,1,0:T(1,128)} %broadcast_in_dim.95), calls=%async_computation.7 | async-start | bytes 16384 | tf_op jit(solution)/shard_map/all_to_all | solution.py:11
  130.5 10.0 %all-to-all-start.8 = ((f32[16,1,4]{2,1,0:T(1,128)}), f32[16,1,4]{2,1,0:T(1,128)S(1)}, u32[]{:S(2)}, u32[]{:S(2)}) async-start(f32[16,1,4]{2,1,0:T(1,128)} %broadcast_in_dim.96), calls=%async_computation.8 | async-start | bytes 16384 | tf_op jit(solution)/shard_map/all_to_all | solution.py:11
  134.7 12.2 %copy-start.1 = (f32[4]{0:T(128)}, f32[4]{0:T(128)S(1)}, u32[]{:S(2)}) copy-start(f32[4]{0:T(128)S(1)} %reduce_sum.204) | copy-start | bytes 52
  142.2 10.8 %all-to-all-start.9 = ((f32[16,1,4096]{2,1,0:T(1,128)}), f32[16,1,4096]{2,1,0:T(1,128)S(1)}, u32[]{:S(2)}, u32[]{:S(2)}) async-start(f32[16,1,4096]{2,1,0:T(1,128)} %reshape.573), calls=%async_computation.9 | async-start | bytes 524288 | tf_op jit(solution)/shard_map/all_to_all | solution.py:11
  154.6 17.9 %copy-start.2 = (f32[4]{0:T(128)S(1)}, f32[4]{0:T(128)}, u32[]{:S(2)}) copy-start(f32[4]{0:T(128)} %copy-done.1) | copy-start | bytes 52
  154.6 17.9 %copy-start.7 = (f32[4]{0:T(128)S(1)}, f32[4]{0:T(128)}, u32[]{:S(2)}) copy-start(f32[4]{0:T(128)} %copy-done.6) | copy-start | bytes 52
  154.7 49.9 %copy-start.13 = (pred[3,3]{1,0:T(4,128)(4,1)S(1)}, pred[3,3]{1,0:T(4,128)(4,1)}, u32[]{:S(2)}) copy-start(pred[3,3]{1,0:T(4,128)(4,1)} %iota_compare_fusion.2) | copy-start | bytes 31
  154.7 50.1 %copy-start.8 = (pred[3,3]{1,0:T(4,128)(4,1)S(1)}, pred[3,3]{1,0:T(4,128)(4,1)}, u32[]{:S(2)}) copy-start(pred[3,3]{1,0:T(4,128)(4,1)} %iota_compare_fusion.3) | copy-start | bytes 31
  158.7 9.8 %all-to-all-start.10 = ((f32[16,1,4]{2,1,0:T(1,128)}), f32[16,1,4]{2,1,0:T(1,128)S(1)}, u32[]{:S(2)}, u32[]{:S(2)}) async-start(f32[16,1,4]{2,1,0:T(1,128)} %broadcast_in_dim.99), calls=%async_computation.10 | async-start | bytes 16384 | tf_op jit(solution)/shard_map/all_to_all | solution.py:11
  169.1 9.8 %all-to-all-start.11 = ((f32[16,1,4]{2,1,0:T(1,128)}), f32[16,1,4]{2,1,0:T(1,128)S(1)}, u32[]{:S(2)}, u32[]{:S(2)}) async-start(f32[16,1,4]{2,1,0:T(1,128)} %broadcast_in_dim.100), calls=%async_computation.11 | async-start | bytes 16384 | tf_op jit(solution)/shard_map/all_to_all | solution.py:11
  179.4 9.8 %all-to-all-start.12 = ((f32[16,1,4]{2,1,0:T(1,128)}), f32[16,1,4]{2,1,0:T(1,128)S(1)}, u32[]{:S(2)}, u32[]{:S(2)}) async-start(f32[16,1,4]{2,1,0:T(1,128)} %broadcast_in_dim.101), calls=%async_computation.12 | async-start | bytes 16384 | tf_op jit(solution)/shard_map/all_to_all | solution.py:11
  189.8 9.8 %all-to-all-start.13 = ((f32[16,1,4]{2,1,0:T(1,128)}), f32[16,1,4]{2,1,0:T(1,128)S(1)}, u32[]{:S(2)}, u32[]{:S(2)}) async-start(f32[16,1,4]{2,1,0:T(1,128)} %broadcast_in_dim.102), calls=%async_computation.13 | async-start | bytes 16384 | tf_op jit(solution)/shard_map/all_to_all | solution.py:11
  (4 other events, 21.4 us)
Sparse Core Ops, SparseCore 0:
  9.2 44.2 all-gather.1
where the time goes:
time: 242 us; the launch traced here: 241 us
  waiting for transfers between devices  71.7 us (30%)
  starting transfers between devices  58.7 us (24%)
  blocking collectives  35.2 us (15%)
  local copies, waits for them, and re-layouts  34.1 us (14%)
  other arithmetic  15.4 us (6%)
  between operations  14 us (6%)
  matrix products  11.5 us (5%)
    all_to_all x12, waiting for transfers between devices, from_everyone(): return lax.all_to_all(copies, axis, split_axis=0, concat_axis=0, tiled=True)  66.9 us
    all_to_all x12, starting transfers between devices, from_everyone(): return lax.all_to_all(copies, axis, split_axis=0, concat_axis=0, tiled=True)  48.7 us
    all_to_all x1, blocking collectives, per_device(): lax.all_to_all(solution, 'grp', split_axis=0, concat_axis=2, tiled=True)  25.4 us
    gather x3, local copies, waits for them, and re-layouts, per_device(): link = inverse[neighbor_table[owner_map]]  14 us
    dot_general x3, matrix products, per_device(): jnp.einsum('sac,scr->sar', op_rows, stacked, precision=lax.Precision.HIGH...  10.1 us
    all_to_all x1, starting transfers between devices, per_device(): lax.all_to_all(right_side, 'grp', split_axis=2, concat_axis=0, tiled=True)  9.97 us
    all_to_all x1, blocking collectives, from_everyone(): return lax.all_to_all(copies, axis, split_axis=0, concat_axis=0, tiled=True)  9.8 us
    unnamed x48, local copies, waits for them, and re-layouts  7.99 us
  transfers between devices with their start and end apart: 14, of which 12 were waited for; matrix products, arithmetic and copies ran while one was open for 13% of the time, Pallas kernels for 0%

commit v1 on v0

--- a/solution.py
+++ b/solution.py
@@ -42,7 +42,15 @@
     )
     link = inverse[neighbor_table[owner_map]]
     op_rows = lax.all_gather(coarse_op, "grp", axis=0, tiled=True)
-    rhs_rows = lax.all_to_all(right_side, "grp", split_axis=2, concat_axis=0, tiled=True)
+    ways, here = (lax.axis_size("grp"), lax.axis_index("grp"))
+    width = right_side.shape[2] // ways
+    turned = jnp.roll(right_side, -here * width, axis=2)
+    got = [lax.slice_in_dim(turned, 0, width, axis=2)]
+    for far in range(1, ways):
+        sent = lax.slice_in_dim(turned, far * width, (far + 1) * width, axis=2)
+        got.append(lax.ppermute(sent, "grp", [(d, (d + far) % ways) for d in range(ways)]))
+    line = jnp.concatenate(got[::-1], axis=0)
+    rhs_rows = jnp.roll(line, (here + 1) * got[0].shape[0], axis=0)
 
     def reduce_sum(values):
         return jax.tree.map(lambda part: over_copies(part, "sub"), values)

time: 242 us -> 257 us (1.062)
  blocking collectives: 35.2 us -> 51.9 us
  starting transfers between devices: 58.7 us -> 72.2 us
  waiting for transfers between devices: 71.7 us -> 62.2 us
  other arithmetic: 15.4 us -> 11.7 us
    ppermute x0 -> x15, starting transfers between devices: none -> 30.2 us  [per_device(): lax.ppermute(sent, 'grp', [(d, (d + far) % ways) for d in range(ways)])]
    all_to_all x1 -> x2, blocking collectives: 9.8 us -> 23 us  [from_everyone(): return lax.all_to_all(copies, axis, split_axis=0, concat_axis=0, tiled=True)]
    all_to_all x1 -> x0, starting transfers between devices: 9.97 us -> none  [per_device(): lax.all_to_all(right_side, 'grp', split_axis=2, concat_axis=0, tiled=True)]
    all_to_all x12 -> x11, waiting for transfers between devices: 66.9 us -> 60.1 us  [from_everyone(): return lax.all_to_all(copies, axis, split_axis=0, concat_axis=0, tiled=True)]
    all_to_all x12 -> x11, starting transfers between devices: 48.7 us -> 42 us  [from_everyone(): return lax.all_to_all(copies, axis, split_axis=0, concat_axis=0, tiled=True)]
    all_to_all x1 -> x0, waiting for transfers between devices: 4.13 us -> none  [per_device(): lax.all_to_all(right_side, 'grp', split_axis=2, concat_axis=0, tiled=True)]
    all_to_all x1, blocking collectives: 25.4 us -> 28.9 us  [per_device(): lax.all_to_all(solution, 'grp', split_axis=0, concat_axis=2, tiled=True)]
    unnamed x48 -> x60, local copies, waits for them, and re-layouts: 7.99 us -> 5.63 us
  transfers between devices with their start and end apart: 14 -> 27, of which waited for: 12 -> 13; matrix products, arithmetic and copies ran while one was open for 13% -> 10% of each run, Pallas kernels for 0% -> 0%
where the time goes in v1:
time: 257 us; the launch traced here: 256 us
  starting transfers between devices  72.2 us (28%)
  waiting for transfers between devices  62.2 us (24%)
  blocking collectives  51.9 us (20%)
  local copies, waits for them, and re-layouts  32.2 us (13%)
  between operations  14.1 us (5%)
  other arithmetic  11.7 us (5%)
  matrix products  11.5 us (4%)
    all_to_all x11, waiting for transfers between devices, from_everyone(): return lax.all_to_all(copies, axis, split_axis=0, concat_axis=0, tiled=True)  60.1 us
    all_to_all x11, starting transfers between devices, from_everyone(): return lax.all_to_all(copies, axis, split_axis=0, concat_axis=0, tiled=True)  42 us
    ppermute x15, starting transfers between devices, per_device(): lax.ppermute(sent, 'grp', [(d, (d + far) % ways) for d in range(ways)])  30.2 us
    all_to_all x1, blocking collectives, per_device(): lax.all_to_all(solution, 'grp', split_axis=0, concat_axis=2, tiled=True)  28.9 us
    all_to_all x2, blocking collectives, from_everyone(): return lax.all_to_all(copies, axis, split_axis=0, concat_axis=0, tiled=True)  23 us
    gather x3, local copies, waits for them, and re-layouts, per_device(): link = inverse[neighbor_table[owner_map]]  14 us
    dot_general x3, matrix products, per_device(): jnp.einsum('sac,scr->sar', op_rows, stacked, precision=lax.Precision.HIGH...  10.1 us
    unnamed x60, local copies, waits for them, and re-layouts  5.63 us
  transfers between devices with their start and end apart: 27, of which 13 were waited for; matrix products, arithmetic and copies ran while one was open for 10% of the time, Pallas kernels for 0%

profile of v1, /device:TPU:1, one launch (start us, length us, event | category | flops | bytes accessed | tf_op | source)
XLA Modules:
  0.0 255.9 jit_solution(8377357582390930401)
XLA Ops:
  10.7 3.9 %collective-permute-start.1 = (f32[1,64,4]{1,2,0:T(4,128)S(1)}, f32[1,64,4]{1,2,0:T(4,128)S(1)}, u32[]{:S(2)}, u32[]{:S(2)}) collective-permute-start(f32[1,64,4]{1,2,0:T(4,128)S(1)} %get-tuple-element.135), channel_id=1, source_target_pairs={{0,224},{16,240},{32,0},{48,16},{64,32},{80,48},{96,64},{112,80},{... | collective-permute-start | bytes 3080 | tf_op jit(solution)/shard_map/ppermute | solution.py:51
  19.1 4.9 %collective-permute-start.5 = (f32[1,64,4]{1,2,0:T(4,128)S(1)}, f32[1,64,4]{1,2,0:T(4,128)S(1)}, u32[]{:S(2)}, u32[]{:S(2)}) collective-permute-start(f32[1,64,4]{1,2,0:T(4,128)S(1)} %get-tuple-element.131), channel_id=1, source_target_pairs={{0,160},{16,176},{32,192},{48,208},{64,224},{80,240},{96,0},{112,1... | collective-permute-start | bytes 3080 | tf_op jit(solution)/shard_map/ppermute | solution.py:51
  25.1 4.5 %collective-permute-start.7 = (f32[1,64,4]{1,2,0:T(4,128)S(1)}, f32[1,64,4]{1,2,0:T(4,128)S(1)}, u32[]{:S(2)}, u32[]{:S(2)}) collective-permute-start(f32[1,64,4]{1,2,0:T(4,128)S(1)} %get-tuple-element.129), channel_id=1, source_target_pairs={{0,128},{16,144},{32,160},{48,176},{64,192},{80,208},{96,224},{112... | collective-permute-start | bytes 3080 | tf_op jit(solution)/shard_map/ppermute | solution.py:51
  43.3 6.8 %all-to-all-start = ((f32[16,1,4]{2,1,0:T(1,128)}), f32[16,1,4]{2,1,0:T(1,128)S(1)}, u32[]{:S(2)}, u32[]{:S(2)}) async-start(f32[16,1,4]{2,1,0:T(1,128)} %broadcast_in_dim.87), calls=%async_computation | async-start | bytes 16384 | tf_op jit(solution)/shard_map/all_to_all | solution.py:11
  50.1 6.4 %all-to-all-done = f32[16,1,4]{2,1,0:T(1,128)S(1)} async-done(((f32[16,1,4]{2,1,0:T(1,128)}), f32[16,1,4]{2,1,0:T(1,128)S(1)}, u32[]{:S(2)}, u32[]{:S(2)}) %all-to-all-start) | async-done | bytes 288 | tf_op jit(solution)/shard_map/all_to_all | solution.py:11
  57.7 3.7 %all-to-all-start.1 = ((f32[16,1,4096]{2,1,0:T(1,128)}), f32[16,1,4096]{2,1,0:T(1,128)S(1)}, u32[]{:S(2)}, u32[]{:S(2)}) async-start(f32[16,1,4096]{2,1,0:T(1,128)} %reshape.567), calls=%async_computation.1 | async-start | bytes 524288 | tf_op jit(solution)/shard_map/all_to_all | solution.py:11
  61.5 13.1 %gather_fusion.1 = s32[2048]{0:T(1024)S(1)} fusion(s32[256]{0:T(256)S(1)} %select_reduce_fusion, s32[2048]{0:T(1024)S(1)} %broadcast_clamp_fusion), kind=kCustom, calls=%fused_computation.1 | custom fusion | bytes 24576 | tf_op jit(solution)/shard_map/gather | solution.py:43
  78.0 4.5 %multiply_reduce_fusion.8 = (f32[4]{0:T(128)S(1)}, f32[4]{0:T(128)S(1)}, f32[16,64,4]{1,2,0:T(4,128)S(1)}) fusion(f32[16,64,4]{1,2,0:T(4,128)S(1)} %dynamic-slice_divide_fusion, f32[16,576,4]{1,2,0:T(4,128)S(1)} %reshape.564, f32[16,64,576]{2,1,0:T(8,128)} %all-gather.2.cloned.1.call-done), kind=kOutput, calls=%fused_computation.66 | convolution fusion | flops 28327928 | bytes 2539552 | tf_op jit(solution)/shard_map/sac,scr->sar/dot_general | solution.py:81
  82.6 12.7 %all_to_all.93 = f32[16,1,4]{2,1,0:T(1,128)S(1)} all-to-all(f32[16,1,4]{2,1,0:T(1,128)S(1)} %broadcast_in_dim.93), channel_id=1, replica_groups=mesh['grp'=16,'sub'=16] {'sub'}, dimensions={0} | all-to-all | bytes 512 | tf_op jit(solution)/shard_map/all_to_all | solution.py:11
  95.8 3.5 %all-to-all-start.3 = ((f32[16,1,4]{2,1,0:T(1,128)}), f32[16,1,4]{2,1,0:T(1,128)S(1)}, u32[]{:S(2)}, u32[]{:S(2)}) async-start(f32[16,1,4]{2,1,0:T(1,128)} %broadcast_in_dim.94), calls=%async_computation.3 | async-start | bytes 16384 | tf_op jit(solution)/shard_map/all_to_all | solution.py:11
  99.3 6.3 %all-to-all-done.3 = f32[16,1,4]{2,1,0:T(1,128)S(1)} async-done(((f32[16,1,4]{2,1,0:T(1,128)}), f32[16,1,4]{2,1,0:T(1,128)S(1)}, u32[]{:S(2)}, u32[]{:S(2)}) %all-to-all-start.3) | async-done | bytes 288 | tf_op jit(solution)/shard_map/all_to_all | solution.py:11
  106.2 10.3 %all_to_all.94 = f32[16,1,4096]{2,1,0:T(1,128)S(1)} all-to-all(f32[16,1,4096]{2,1,0:T(1,128)S(1)} %reshape.569), channel_id=1, replica_groups=mesh['grp'=16,'sub'=16] {'sub'}, dimensions={0} | all-to-all | bytes 524288 | tf_op jit(solution)/shard_map/all_to_all | solution.py:11
  122.0 3.5 %all-to-all-start.5 = ((f32[16,1,4]{2,1,0:T(1,128)}), f32[16,1,4]{2,1,0:T(1,128)S(1)}, u32[]{:S(2)}, u32[]{:S(2)}) async-start(f32[16,1,4]{2,1,0:T(1,128)} %broadcast_in_dim.97), calls=%async_computation.5 | async-start | bytes 16384 | tf_op jit(solution)/shard_map/all_to_all | solution.py:11
  126.2 5.6 %all-to-all-done.5 = f32[16,1,4]{2,1,0:T(1,128)S(1)} async-done(((f32[16,1,4]{2,1,0:T(1,128)}), f32[16,1,4]{2,1,0:T(1,128)S(1)}, u32[]{:S(2)}, u32[]{:S(2)}) %all-to-all-start.5) | async-done | bytes 288 | tf_op jit(solution)/shard_map/all_to_all | solution.py:11
  135.9 6.3 %all-to-all-done.6 = f32[16,1,4]{2,1,0:T(1,128)S(1)} async-done(((f32[16,1,4]{2,1,0:T(1,128)}), f32[16,1,4]{2,1,0:T(1,128)S(1)}, u32[]{:S(2)}, u32[]{:S(2)}) %all-to-all-start.6) | async-done | bytes 288 | tf_op jit(solution)/shard_map/all_to_all | solution.py:11
  146.4 6.2 %all-to-all-done.7 = f32[16,1,4]{2,1,0:T(1,128)S(1)} async-done(((f32[16,1,4]{2,1,0:T(1,128)}), f32[16,1,4]{2,1,0:T(1,128)S(1)}, u32[]{:S(2)}, u32[]{:S(2)}) %all-to-all-start.7) | async-done | bytes 288 | tf_op jit(solution)/shard_map/all_to_all | solution.py:11
  153.8 3.8 %all-to-all-start.8 = ((f32[16,1,4096]{2,1,0:T(1,128)}), f32[16,1,4096]{2,1,0:T(1,128)S(1)}, u32[]{:S(2)}, u32[]{:S(2)}) async-start(f32[16,1,4096]{2,1,0:T(1,128)} %reshape.571), calls=%async_computation.8 | async-start | bytes 524288 | tf_op jit(solution)/shard_map/all_to_all | solution.py:11
  159.0 5.6 %all-to-all-done.8 = f32[16,1,4096]{2,1,0:T(1,128)S(1)} async-done(((f32[16,1,4096]{2,1,0:T(1,128)}), f32[16,1,4096]{2,1,0:T(1,128)S(1)}, u32[]{:S(2)}, u32[]{:S(2)}) %all-to-all-start.8) | async-done | bytes 262176 | tf_op jit(solution)/shard_map/all_to_all | solution.py:11
  170.2 3.5 %all-to-all-start.9 = ((f32[16,1,4]{2,1,0:T(1,128)}), f32[16,1,4]{2,1,0:T(1,128)S(1)}, u32[]{:S(2)}, u32[]{:S(2)}) async-start(f32[16,1,4]{2,1,0:T(1,128)} %broadcast_in_dim.102), calls=%async_computation.9 | async-start | bytes 16384 | tf_op jit(solution)/shard_map/all_to_all | solution.py:11
  173.7 6.2 %all-to-all-done.9 = f32[16,1,4]{2,1,0:T(1,128)S(1)} async-done(((f32[16,1,4]{2,1,0:T(1,128)}), f32[16,1,4]{2,1,0:T(1,128)S(1)}, u32[]{:S(2)}, u32[]{:S(2)}) %all-to-all-start.9) | async-done | bytes 288 | tf_op jit(solution)/shard_map/all_to_all | solution.py:11
  184.0 6.3 %all-to-all-done.10 = f32[16,1,4]{2,1,0:T(1,128)S(1)} async-done(((f32[16,1,4]{2,1,0:T(1,128)}), f32[16,1,4]{2,1,0:T(1,128)S(1)}, u32[]{:S(2)}, u32[]{:S(2)}) %all-to-all-start.10) | async-done | bytes 288 | tf_op jit(solution)/shard_map/all_to_all | solution.py:11
  195.7 5.0 %all-to-all-done.11 = f32[16,1,4]{2,1,0:T(1,128)S(1)} async-done(((f32[16,1,4]{2,1,0:T(1,128)}), f32[16,1,4]{2,1,0:T(1,128)S(1)}, u32[]{:S(2)}, u32[]{:S(2)}) %all-to-all-start.11) | async-done | bytes 288 | tf_op jit(solution)/shard_map/all_to_all | solution.py:11
  204.9 6.2 %all-to-all-done.12 = f32[16,1,4]{2,1,0:T(1,128)S(1)} async-done(((f32[16,1,4]{2,1,0:T(1,128)}), f32[16,1,4]{2,1,0:T(1,128)S(1)}, u32[]{:S(2)}, u32[]{:S(2)}) %all-to-all-start.12) | async-done | bytes 288 | tf_op jit(solution)/shard_map/all_to_all | solution.py:11
  218.7 28.9 %all_to_all.95 = f32[16,1,256]{2,1,0:T(1,128)S(1)} all-to-all(f32[16,1,256]{2,1,0:T(1,128)S(1)} %reshape.573), channel_id=1, replica_groups=mesh['grp'=16,'sub'=16] {'grp'}, dimensions={0} | all-to-all | bytes 32768 | tf_op jit(solution)/shard_map/all_to_all | solution.py:103
  (195 shorter events, 74.3 us)
Async XLA Ops:
  6.5 71.5 %all-gather.2.cloned.1.call-start = ((), (), s32[]{:S(2)}) async-start(), calls=%async_computation.14 | async-start | bytes 2785280 | tf_op jit(solution)/shard_map/all_gather | solution.py:44
  7.4 11.7 %collective-permute-start = (f32[1,64,4]{1,2,0:T(4,128)S(1)}, f32[1,64,4]{1,2,0:T(4,128)S(1)}, u32[]{:S(2)}, u32[]{:S(2)}) collective-permute-start(f32[1,64,4]{1,2,0:T(4,128)S(1)} %get-tuple-element.136), channel_id=1, source_target_pairs={{0,240},{16,0},{32,16},{48,32},{64,48},{80,64},{96,80},{112,96},{1... | collective-permute-start | bytes 3080 | tf_op jit(solution)/shard_map/ppermute | solution.py:51
  10.7 13.4 %collective-permute-start.1 = (f32[1,64,4]{1,2,0:T(4,128)S(1)}, f32[1,64,4]{1,2,0:T(4,128)S(1)}, u32[]{:S(2)}, u32[]{:S(2)}) collective-permute-start(f32[1,64,4]{1,2,0:T(4,128)S(1)} %get-tuple-element.135), channel_id=1, source_target_pairs={{0,224},{16,240},{32,0},{48,16},{64,32},{80,48},{96,64},{112,80},{... | collective-permute-start | bytes 3080 | tf_op jit(solution)/shard_map/ppermute | solution.py:51
  14.5 10.6 %collective-permute-start.2 = (f32[1,64,4]{1,2,0:T(4,128)S(1)}, f32[1,64,4]{1,2,0:T(4,128)S(1)}, u32[]{:S(2)}, u32[]{:S(2)}) collective-permute-start(f32[1,64,4]{1,2,0:T(4,128)S(1)} %get-tuple-element.134), channel_id=1, source_target_pairs={{0,208},{16,224},{32,240},{48,0},{64,16},{80,32},{96,48},{112,64},... | collective-permute-start | bytes 3080 | tf_op jit(solution)/shard_map/ppermute | solution.py:51
  15.9 13.7 %collective-permute-start.3 = (f32[1,64,4]{1,2,0:T(4,128)S(1)}, f32[1,64,4]{1,2,0:T(4,128)S(1)}, u32[]{:S(2)}, u32[]{:S(2)}) collective-permute-start(f32[1,64,4]{1,2,0:T(4,128)S(1)} %get-tuple-element.133), channel_id=1, source_target_pairs={{0,192},{16,208},{32,224},{48,240},{64,0},{80,16},{96,32},{112,48}... | collective-permute-start | bytes 3080 | tf_op jit(solution)/shard_map/ppermute | solution.py:51
  16.7 14.2 %collective-permute-start.4 = (f32[1,64,4]{1,2,0:T(4,128)S(1)}, f32[1,64,4]{1,2,0:T(4,128)S(1)}, u32[]{:S(2)}, u32[]{:S(2)}) collective-permute-start(f32[1,64,4]{1,2,0:T(4,128)S(1)} %get-tuple-element.132), channel_id=1, source_target_pairs={{0,176},{16,192},{32,208},{48,224},{64,240},{80,0},{96,16},{112,32... | collective-permute-start | bytes 3080 | tf_op jit(solution)/shard_map/ppermute | solution.py:51
  19.1 14.6 %collective-permute-start.5 = (f32[1,64,4]{1,2,0:T(4,128)S(1)}, f32[1,64,4]{1,2,0:T(4,128)S(1)}, u32[]{:S(2)}, u32[]{:S(2)}) collective-permute-start(f32[1,64,4]{1,2,0:T(4,128)S(1)} %get-tuple-element.131), channel_id=1, source_target_pairs={{0,160},{16,176},{32,192},{48,208},{64,224},{80,240},{96,0},{112,1... | collective-permute-start | bytes 3080 | tf_op jit(solution)/shard_map/ppermute | solution.py:51
  24.0 12.3 %collective-permute-start.6 = (f32[1,64,4]{1,2,0:T(4,128)S(1)}, f32[1,64,4]{1,2,0:T(4,128)S(1)}, u32[]{:S(2)}, u32[]{:S(2)}) collective-permute-start(f32[1,64,4]{1,2,0:T(4,128)S(1)} %get-tuple-element.130), channel_id=1, source_target_pairs={{0,144},{16,160},{32,176},{48,192},{64,208},{80,224},{96,240},{112... | collective-permute-start | bytes 3080 | tf_op jit(solution)/shard_map/ppermute | solution.py:51
  25.1 11.2 %collective-permute-start.7 = (f32[1,64,4]{1,2,0:T(4,128)S(1)}, f32[1,64,4]{1,2,0:T(4,128)S(1)}, u32[]{:S(2)}, u32[]{:S(2)}) collective-permute-start(f32[1,64,4]{1,2,0:T(4,128)S(1)} %get-tuple-element.129), channel_id=1, source_target_pairs={{0,128},{16,144},{32,160},{48,176},{64,192},{80,208},{96,224},{112... | collective-permute-start | bytes 3080 | tf_op jit(solution)/shard_map/ppermute | solution.py:51
  29.6 8.7 %collective-permute-start.8 = (f32[1,64,4]{1,2,0:T(4,128)S(1)}, f32[1,64,4]{1,2,0:T(4,128)S(1)}, u32[]{:S(2)}, u32[]{:S(2)}) collective-permute-start(f32[1,64,4]{1,2,0:T(4,128)S(1)} %get-tuple-element.128), channel_id=1, source_target_pairs={{0,112},{16,128},{32,144},{48,160},{64,176},{80,192},{96,208},{112... | collective-permute-start | bytes 3080 | tf_op jit(solution)/shard_map/ppermute | solution.py:51
  30.9 8.9 %collective-permute-start.9 = (f32[1,64,4]{1,2,0:T(4,128)S(1)}, f32[1,64,4]{1,2,0:T(4,128)S(1)}, u32[]{:S(2)}, u32[]{:S(2)}) collective-permute-start(f32[1,64,4]{1,2,0:T(4,128)S(1)} %get-tuple-element.127), channel_id=1, source_target_pairs={{0,96},{16,112},{32,128},{48,144},{64,160},{80,176},{96,192},{112,... | collective-permute-start | bytes 3080 | tf_op jit(solution)/shard_map/ppermute | solution.py:51
  33.7 6.6 %collective-permute-start.10 = (f32[1,64,4]{1,2,0:T(4,128)S(1)}, f32[1,64,4]{1,2,0:T(4,128)S(1)}, u32[]{:S(2)}, u32[]{:S(2)}) collective-permute-start(f32[1,64,4]{1,2,0:T(4,128)S(1)} %get-tuple-element.126), channel_id=1, source_target_pairs={{0,80},{16,96},{32,112},{48,128},{64,144},{80,160},{96,176},{112,1... | collective-permute-start | bytes 3080 | tf_op jit(solution)/shard_map/ppermute | solution.py:51
  36.3 4.7 %collective-permute-start.12 = (f32[1,64,4]{1,2,0:T(4,128)S(1)}, f32[1,64,4]{1,2,0:T(4,128)S(1)}, u32[]{:S(2)}, u32[]{:S(2)}) collective-permute-start(f32[1,64,4]{1,2,0:T(4,128)S(1)} %get-tuple-element.124), channel_id=1, source_target_pairs={{0,48},{16,64},{32,80},{48,96},{64,112},{80,128},{96,144},{112,160... | collective-permute-start | bytes 3080 | tf_op jit(solution)/shard_map/ppermute | solution.py:51
  43.3 13.1 %all-to-all-start = ((f32[16,1,4]{2,1,0:T(1,128)}), f32[16,1,4]{2,1,0:T(1,128)S(1)}, u32[]{:S(2)}, u32[]{:S(2)}) async-start(f32[16,1,4]{2,1,0:T(1,128)} %broadcast_in_dim.87), calls=%async_computation | async-start | bytes 16384 | tf_op jit(solution)/shard_map/all_to_all | solution.py:11
  57.7 17.7 %all-to-all-start.1 = ((f32[16,1,4096]{2,1,0:T(1,128)}), f32[16,1,4096]{2,1,0:T(1,128)S(1)}, u32[]{:S(2)}, u32[]{:S(2)}) async-start(f32[16,1,4096]{2,1,0:T(1,128)} %reshape.567), calls=%async_computation.1 | async-start | bytes 524288 | tf_op jit(solution)/shard_map/all_to_all | solution.py:11
  95.8 9.8 %all-to-all-start.3 = ((f32[16,1,4]{2,1,0:T(1,128)}), f32[16,1,4]{2,1,0:T(1,128)S(1)}, u32[]{:S(2)}, u32[]{:S(2)}) async-start(f32[16,1,4]{2,1,0:T(1,128)} %broadcast_in_dim.94), calls=%async_computation.3 | async-start | bytes 16384 | tf_op jit(solution)/shard_map/all_to_all | solution.py:11
  122.0 9.8 %all-to-all-start.5 = ((f32[16,1,4]{2,1,0:T(1,128)}), f32[16,1,4]{2,1,0:T(1,128)S(1)}, u32[]{:S(2)}, u32[]{:S(2)}) async-start(f32[16,1,4]{2,1,0:T(1,128)} %broadcast_in_dim.97), calls=%async_computation.5 | async-start | bytes 16384 | tf_op jit(solution)/shard_map/all_to_all | solution.py:11
  132.4 9.8 %all-to-all-start.6 = ((f32[16,1,4]{2,1,0:T(1,128)}), f32[16,1,4]{2,1,0:T(1,128)S(1)}, u32[]{:S(2)}, u32[]{:S(2)}) async-start(f32[16,1,4]{2,1,0:T(1,128)} %broadcast_in_dim.98), calls=%async_computation.6 | async-start | bytes 16384 | tf_op jit(solution)/shard_map/all_to_all | solution.py:11
  142.8 9.8 %all-to-all-start.7 = ((f32[16,1,4]{2,1,0:T(1,128)}), f32[16,1,4]{2,1,0:T(1,128)S(1)}, u32[]{:S(2)}, u32[]{:S(2)}) async-start(f32[16,1,4]{2,1,0:T(1,128)} %broadcast_in_dim.99), calls=%async_computation.7 | async-start | bytes 16384 | tf_op jit(solution)/shard_map/all_to_all | solution.py:11
  153.8 10.8 %all-to-all-start.8 = ((f32[16,1,4096]{2,1,0:T(1,128)}), f32[16,1,4096]{2,1,0:T(1,128)S(1)}, u32[]{:S(2)}, u32[]{:S(2)}) async-start(f32[16,1,4096]{2,1,0:T(1,128)} %reshape.571), calls=%async_computation.8 | async-start | bytes 524288 | tf_op jit(solution)/shard_map/all_to_all | solution.py:11
  170.2 9.8 %all-to-all-start.9 = ((f32[16,1,4]{2,1,0:T(1,128)}), f32[16,1,4]{2,1,0:T(1,128)S(1)}, u32[]{:S(2)}, u32[]{:S(2)}) async-start(f32[16,1,4]{2,1,0:T(1,128)} %broadcast_in_dim.102), calls=%async_computation.9 | async-start | bytes 16384 | tf_op jit(solution)/shard_map/all_to_all | solution.py:11
  180.5 9.8 %all-to-all-start.10 = ((f32[16,1,4]{2,1,0:T(1,128)}), f32[16,1,4]{2,1,0:T(1,128)S(1)}, u32[]{:S(2)}, u32[]{:S(2)}) async-start(f32[16,1,4]{2,1,0:T(1,128)} %broadcast_in_dim.103), calls=%async_computation.10 | async-start | bytes 16384 | tf_op jit(solution)/shard_map/all_to_all | solution.py:11
  190.9 9.8 %all-to-all-start.11 = ((f32[16,1,4]{2,1,0:T(1,128)}), f32[16,1,4]{2,1,0:T(1,128)S(1)}, u32[]{:S(2)}, u32[]{:S(2)}) async-start(f32[16,1,4]{2,1,0:T(1,128)} %broadcast_in_dim.104), calls=%async_computation.11 | async-start | bytes 16384 | tf_op jit(solution)/shard_map/all_to_all | solution.py:11
  201.3 9.8 %all-to-all-start.12 = ((f32[16,1,4]{2,1,0:T(1,128)}), f32[16,1,4]{2,1,0:T(1,128)S(1)}, u32[]{:S(2)}, u32[]{:S(2)}) async-start(f32[16,1,4]{2,1,0:T(1,128)} %broadcast_in_dim.105), calls=%async_computation.12 | async-start | bytes 16384 | tf_op jit(solution)/shard_map/all_to_all | solution.py:11
  (9 other events, 268.2 us)
Sparse Core Ops, SparseCore 0:
  16.8 41.6 all-gather.1
